TPU v7x, 32 devices: a whole 2x2x4 slice. The times are simulated.
32 devices in a mesh: dp: 8 (over z, y), tensor: 4 (over x, core).
Axes of the slice: x: 2, y: 2, z: 4, core: 2. Of those that a mesh axis runs over, the one named last changes fastest.
Arguments:
- acts: bfloat16 [8, 2048, 1024], P('dp', 'tensor'), may hold values from -6 to 6
- grad_out: bfloat16 [8, 2048, 1024], P('dp', 'tensor'), may hold values from -6 to 6
- norm_gain: float32 [1024], replicated, may hold values from 0.5 to 1.5
- w_zx: bfloat16 [1024, 2, 2048], P('dp', None, 'tensor'), may hold values from -0.1875 to 0.1875
- w_bc: bfloat16 [1024, 256], P('dp'), may hold values from -0.1875 to 0.1875
- w_dt: bfloat16 [1024, 32], P('dp', 'tensor'), may hold values from -0.1875 to 0.1875
- w_out: bfloat16 [1024, 2048], P('dp', 'tensor'), may hold values from -0.125 to 0.125
- conv_x: float32 [4, 2048], replicated, may hold values from -3 to 3
- conv_x_bias: float32 [2048], replicated, may hold values from -0.5 to 0.5
- conv_bc: float32 [4, 256], replicated, may hold values from -3 to 3
- conv_bc_bias: float32 [256], replicated, may hold values from -0.5 to 0.5
- dt_bias: float32 [32], replicated, may hold values from -7 to -2
- a_log: float32 [32], replicated, may hold values from 0 to 2.77
- d_skip: float32 [32], replicated, may hold values from 0.5 to 1.5
- gate_gain: float32 [2048], replicated, may hold values from 0.5 to 1.5
Outputs:
- out_acts: bfloat16 [8, 2048, 1024], P('dp', 'tensor')
- grad_acts: float32 [8, 2048, 1024], P('dp', 'tensor')
- grad_norm_gain: float32 [1024], replicated
- grad_w_zx: float32 [1024, 2, 2048], P('dp', None, 'tensor')
- grad_w_bc: float32 [1024, 256], P('dp')
- grad_w_dt: float32 [1024, 32], P('dp', 'tensor')
- grad_w_out: float32 [1024, 2048], P('dp', 'tensor')
- grad_conv_x: float32 [4, 2048], replicated
- grad_conv_x_bias: float32 [2048], replicated
- grad_conv_bc: float32 [4, 256], replicated
- grad_conv_bc_bias: float32 [256], replicated
- grad_dt_bias: float32 [32], replicated
- grad_a_log: float32 [32], replicated
- grad_d_skip: float32 [32], replicated
- grad_gate_gain: float32 [2048], replicated
All inputs are finite; a program needn't handle non-finite values.
Results may differ from a plain program's by a relative error of at most 0.0096.
Values may be sent and summed in bfloat16 or wider, within the bound.
A program may use at most 192 MiB of HBM per device.

v0:
```python
import jax
import jax.numpy as jnp
from jax import lax
from jax.sharding import PartitionSpec as P

BLOCK_LEN = 256
EPSILON = 1e-05
FULL_PRECISION = lax.Precision.HIGHEST
CONTRACT_LAST = (((1,), (1,)), ((), ()))
CONTRACT_FIRST = (((0,), (0,)), ((), ()))


def causal_conv(values, conv_taps):
    tap_count = conv_taps.shape[0]
    length = values.shape[0]
    padded = jnp.pad(values, ((tap_count - 1, 0), (0, 0)))
    result = conv_taps[0] * padded[0:length]
    for offset in range(1, tap_count):
        result = result + conv_taps[offset] * padded[offset : offset + length]
    return result


def ssd_scan(x_heads, step_dt, decay_rate, b_mat, c_mat, block_size):
    length, head_count, head_width = x_heads.shape
    state_count = b_mat.shape[1]
    block_count = length // block_size
    x_blocks = x_heads.reshape(block_count, block_size, head_count, head_width)
    dt_blocks = step_dt.reshape(block_count, block_size, head_count)
    b_blocks = b_mat.reshape(block_count, block_size, state_count)
    c_blocks = c_mat.reshape(block_count, block_size, state_count)
    positions = jnp.arange(block_size)
    causal_mask = (positions[:, None] >= positions[None, :]).astype(jnp.float32)

    def step_block(state, inputs):
        x_block, dt_block, b_block, c_block = inputs
        cum_logs = jnp.cumsum(dt_block * decay_rate[None, :], axis=0)
        scores = jnp.dot(c_block, b_block.T, precision=FULL_PRECISION)
        log_gaps = (cum_logs[:, None, :] - cum_logs[None, :, :]) * causal_mask[:, :, None]
        weights = (
            scores[:, :, None] * jnp.exp(log_gaps) * causal_mask[:, :, None] * dt_block[None, :, :]
        )
        within = jnp.einsum("ijh,jhp->ihp", weights, x_block, precision=FULL_PRECISION)
        carried = (
            jnp.einsum("in,hpn->ihp", c_block, state, precision=FULL_PRECISION)
            * jnp.exp(cum_logs)[:, :, None]
        )
        block_total = cum_logs[-1]
        state_weight = jnp.exp(block_total[None, :] - cum_logs) * dt_block
        update = jnp.einsum(
            "jhp,jn->hpn", x_block * state_weight[:, :, None], b_block, precision=FULL_PRECISION
        )
        new_state = state * jnp.exp(block_total)[:, None, None] + update
        return (new_state, within + carried)

    zero_state = jnp.zeros((head_count, head_width, state_count), jnp.float32)
    final_state, outputs = lax.scan(
        jax.checkpoint(step_block), zero_state, (x_blocks, dt_blocks, b_blocks, c_blocks)
    )
    return outputs.reshape(length, head_count, head_width)


def pre_norm(acts_row, norm_gain):
    return (
        acts_row
        * lax.rsqrt(jnp.mean(acts_row * acts_row, axis=-1, keepdims=True) + EPSILON)
        * norm_gain
    )


def conv_part(x_vals, bc_vals, x_taps, x_shift, bc_taps, bc_shift):
    x_conv = jax.nn.silu(causal_conv(x_vals, x_taps) + x_shift)
    bc_conv = jax.nn.silu(causal_conv(bc_vals, bc_taps) + bc_shift)
    return (x_conv, bc_conv)


def mix_part(x_vals, b_vals, c_vals, dt_vals, dt_shift, log_rate, skip_gain, gate_vals):
    length = x_vals.shape[0]
    head_count = dt_vals.shape[1]
    x_heads = x_vals.reshape(length, head_count, -1)
    step_dt = jax.nn.softplus(dt_vals + dt_shift)
    mixed = (
        ssd_scan(x_heads, step_dt, -jnp.exp(log_rate), b_vals, c_vals, BLOCK_LEN)
        + skip_gain[None, :, None] * x_heads
    )
    return mixed.reshape(length, -1) * jax.nn.silu(gate_vals)


def widen(piece, start, full_size):
    holder = jnp.zeros(piece.shape[:-1] + (full_size,), jnp.float32)
    return lax.dynamic_update_slice_in_dim(holder, piece, start, piece.ndim - 1)


def body(
    acts,
    grad_out,
    norm_gain,
    w_zx,
    w_bc,
    w_dt,
    w_out,
    conv_x,
    conv_x_bias,
    conv_bc,
    conv_bc_bias,
    dt_bias,
    a_log,
    d_skip,
    gate_gain,
):
    parts = lax.axis_size("tensor")
    rank = lax.axis_index("tensor")
    local_rows = acts.shape[1]
    channels = w_zx.shape[2]
    head_count = w_dt.shape[1]
    state_count = w_bc.shape[1] // 2
    total_channels = channels * parts
    total_heads = head_count * parts
    chan_start = rank * channels
    head_start = rank * head_count
    zx_full, bc_full, dt_full, out_full = (
        lax.all_gather(w_zx, "dp", axis=0, tiled=True),
        lax.all_gather(w_bc, "dp", axis=0, tiled=True),
        lax.all_gather(w_dt, "dp", axis=0, tiled=True),
        lax.all_gather(w_out, "dp", axis=0, tiled=True),
    )
    acts_row = acts[0].astype(jnp.float32)
    normed_in, pre_back = jax.vjp(pre_norm, acts_row, norm_gain)
    hidden = lax.all_gather(normed_in.astype(jnp.bfloat16), "tensor", axis=0, tiled=True)
    zx_proj = jnp.einsum("ld,dkc->lkc", hidden, zx_full, preferred_element_type=jnp.float32)
    bc_proj = jnp.dot(hidden, bc_full, preferred_element_type=jnp.float32)
    dt_proj = jnp.dot(hidden, dt_full, preferred_element_type=jnp.float32)
    conv_x_local = lax.dynamic_slice_in_dim(conv_x, chan_start, channels, 1)
    conv_xb_local = lax.dynamic_slice_in_dim(conv_x_bias, chan_start, channels, 0)
    dt_bias_local = lax.dynamic_slice_in_dim(dt_bias, head_start, head_count, 0)
    a_log_local = lax.dynamic_slice_in_dim(a_log, head_start, head_count, 0)
    d_skip_local = lax.dynamic_slice_in_dim(d_skip, head_start, head_count, 0)
    gain_local = lax.dynamic_slice_in_dim(gate_gain, chan_start, channels, 0)
    conv_outs, conv_back = jax.vjp(
        conv_part, zx_proj[:, 1], bc_proj, conv_x_local, conv_xb_local, conv_bc, conv_bc_bias
    )
    x_conv, bc_conv = conv_outs
    x_low = x_conv.astype(jnp.bfloat16)
    b_low = bc_conv[:, :state_count].astype(jnp.bfloat16)
    c_low = bc_conv[:, state_count:].astype(jnp.bfloat16)
    gated, mix_back = jax.vjp(
        mix_part,
        x_low.astype(jnp.float32),
        b_low.astype(jnp.float32),
        c_low.astype(jnp.float32),
        dt_proj,
        dt_bias_local,
        a_log_local,
        d_skip_local,
        zx_proj[:, 0],
    )
    square_total = lax.psum(jnp.sum(gated * gated, axis=1), "tensor")
    inv_rms = lax.rsqrt(square_total / total_channels + EPSILON)[:, None]
    mixed_out = (gated * inv_rms * gain_local).astype(jnp.bfloat16)
    projected = lax.psum_scatter(
        lax.dot_general(mixed_out, out_full, CONTRACT_LAST, preferred_element_type=jnp.float32),
        "tensor",
        scatter_dimension=0,
        tiled=True,
    )
    out_acts = (acts_row + projected).astype(jnp.bfloat16)[None]
    grad_row = grad_out[0]
    grad_rows_all = lax.all_gather(grad_row, "tensor", axis=0, tiled=True)
    grad_mixed = jnp.dot(grad_rows_all, out_full, preferred_element_type=jnp.float32).astype(
        jnp.bfloat16
    )
    grad_out_w = lax.dot_general(
        grad_rows_all, mixed_out, CONTRACT_FIRST, preferred_element_type=jnp.float32
    )
    grad_normed = grad_mixed.astype(jnp.float32)
    grad_gain_local = jnp.sum(grad_normed * gated * inv_rms, axis=0)
    scaled = grad_normed * gain_local
    row_dot = lax.psum(jnp.sum(scaled * gated, axis=1), "tensor")
    grad_gated = (
        inv_rms * scaled
        - gated * (inv_rms * inv_rms * inv_rms) * (row_dot / total_channels)[:, None]
    )
    (
        grad_x_low,
        grad_b,
        grad_c,
        grad_dt_in,
        grad_dt_shift,
        grad_log_rate,
        grad_skip,
        grad_gate_in,
    ) = mix_back(grad_gated)
    grad_x_in, grad_bc_part, grad_x_taps, grad_x_shift, grad_bc_taps, grad_bc_shift = conv_back(
        (grad_x_low, jnp.concatenate([grad_b, grad_c], axis=1))
    )
    grad_bc_in = lax.psum(grad_bc_part, "tensor").astype(jnp.bfloat16)
    grad_zx = jnp.stack([grad_gate_in.astype(jnp.bfloat16), grad_x_in.astype(jnp.bfloat16)], axis=1)
    grad_dt_low = grad_dt_in.astype(jnp.bfloat16)
    grad_zx_w = jnp.einsum("ld,lkc->dkc", hidden, grad_zx, preferred_element_type=jnp.float32)
    grad_bc_w = lax.dot_general(
        hidden, grad_bc_in, CONTRACT_FIRST, preferred_element_type=jnp.float32
    )
    grad_dt_w = lax.dot_general(
        hidden, grad_dt_low, CONTRACT_FIRST, preferred_element_type=jnp.float32
    )
    from_zx = jnp.einsum("lkc,dkc->ld", grad_zx, zx_full, preferred_element_type=jnp.float32)
    grad_hidden = lax.psum_scatter(
        from_zx
        + lax.dot_general(grad_dt_low, dt_full, CONTRACT_LAST, preferred_element_type=jnp.float32),
        "tensor",
        scatter_dimension=0,
        tiled=True,
    )
    bc_piece = lax.dynamic_slice_in_dim(grad_bc_in, rank * local_rows, local_rows, 0)
    grad_hidden = grad_hidden + lax.dot_general(
        bc_piece, bc_full, CONTRACT_LAST, preferred_element_type=jnp.float32
    )
    grad_acts_norm, grad_norm_gain = pre_back(grad_hidden)
    grad_acts = (grad_row.astype(jnp.float32) + grad_acts_norm)[None]
    grad_w_zx, grad_w_bc, grad_w_dt, grad_w_out = (
        lax.psum_scatter(grad_zx_w, "dp", scatter_dimension=0, tiled=True),
        lax.psum_scatter(grad_bc_w, "dp", scatter_dimension=0, tiled=True),
        lax.psum_scatter(grad_dt_w, "dp", scatter_dimension=0, tiled=True),
        lax.psum_scatter(grad_out_w, "dp", scatter_dimension=0, tiled=True),
    )
    small_sums = lax.psum(
        (
            grad_norm_gain,
            widen(grad_x_taps, chan_start, total_channels),
            widen(grad_x_shift, chan_start, total_channels),
            grad_bc_taps,
            grad_bc_shift,
            widen(grad_dt_shift, head_start, total_heads),
            widen(grad_log_rate, head_start, total_heads),
            widen(grad_skip, head_start, total_heads),
            widen(grad_gain_local, chan_start, total_channels),
        ),
        ("dp", "tensor"),
    )
    grad_ng, grad_cx, grad_cxb, grad_cbc, grad_cbcb, grad_dtb, grad_alog, grad_dsk, grad_gg = (
        small_sums
    )
    return (
        out_acts,
        grad_acts,
        grad_ng,
        grad_w_zx,
        grad_w_bc,
        grad_w_dt,
        grad_w_out,
        grad_cx,
        grad_cxb,
        grad_cbc,
        grad_cbcb,
        grad_dtb,
        grad_alog,
        grad_dsk,
        grad_gg,
    )


def solution(mesh):
    in_specs = (
        P("dp", "tensor", None),
        P("dp", "tensor", None),
        P(),
        P("dp", None, "tensor"),
        P("dp", None),
        P("dp", "tensor"),
        P("dp", "tensor"),
        P(),
        P(),
        P(),
        P(),
        P(),
        P(),
        P(),
        P(),
    )
    out_specs = (
        P("dp", "tensor", None),
        P("dp", "tensor", None),
        P(),
        P("dp", None, "tensor"),
        P("dp", None),
        P("dp", "tensor"),
        P("dp", "tensor"),
        P(),
        P(),
        P(),
        P(),
        P(),
        P(),
        P(),
        P(),
    )
    return jax.shard_map(body, mesh=mesh, in_specs=in_specs, out_specs=out_specs, check_vma=False)
```

profile of v0, /device:TPU:0, one launch (start us, length us, event | category | flops | bytes accessed | tf_op | source)
XLA Modules:
  0.0 918.6 jit_solution(7278153467009917441)
XLA Ops:
  16.2 27.9 %all_gather.19 = bf16[1024,8]{0,1:T(8,128)(2,1)S(1)} all-gather(bf16[128,8]{0,1:T(8,128)(2,1)S(1)} %copy-done.49), channel_id=1, replica_groups=mesh['dp'=8,'tensor'=4] {'dp'}, dimensions={0}, use_global_device_ids=true | all-gather | bytes 18432 | tf_op jit(solution)/shard_map/all_gather | solution.py:123
  44.2 32.4 %all_gather.21 = bf16[1024,256]{1,0:T(8,128)(2,1)S(1)} all-gather(bf16[128,256]{1,0:T(8,128)(2,1)S(1)} %copy-done.20), channel_id=1, replica_groups=mesh['dp'=8,'tensor'=4] {'dp'}, dimensions={0}, use_global_device_ids=true | all-gather | bytes 589824 | tf_op jit(solution)/shard_map/all_gather | solution.py:122
  77.6 3.8 fusion.161
  86.3 15.2 %all-gather.8.cloned.1.call-done = bf16[1024,2,512]{2,0,1:T(8,128)(2,1)} async-done(((bf16[128,2,512]{2,0,1:T(8,128)(2,1)}), bf16[1024,2,512]{2,0,1:T(8,128)(2,1)}) %all-gather.8.cloned.1.call-update) | async-done | bytes 2097168 | tf_op jit(solution)/shard_map/all_gather | solution.py:121
  101.5 7.1 fusion.109
  112.3 4.7 fusion.123
  117.0 7.1 reshape.372
  124.1 6.9 copy.89
  130.9 4.0 compare_select_fusion.2
  137.4 87.5 %while.43 = (s32[]{:T(128)}, f32[8,64,128]{2,1,0:T(8,128)S(1)}, f32[8,256,8,64]{1,3,2,0:T(8,128)}, f32[8,8,64,128]{3,2,1,0:T(8,128)}, f32[8,256,8]{1,2,0:T(8,128...) while((s32[]{:T(128)}, f32[8,64,128]{2,1,0:T(8,128)S(1)}, ...), condition=%wide.region_4.5_spmd.clone.clone, body=%wide.region_1.4_spmd.clone.clone.sunk | while | flops 909711360 | bytes 5641051 | solution.py:56
  140.0 3.6 fusion.270
  150.9 3.6 fusion.270
  161.9 3.6 fusion.270
  172.9 3.6 fusion.270
  183.8 3.6 fusion.270
  194.7 3.6 fusion.270
  205.7 3.6 fusion.270
  216.6 3.6 fusion.270
  225.0 6.9 copy.101
  231.9 7.5 reshape.369
  239.4 7.6 multiply_reduce_fusion.8
  246.9 5.7 psum.84
  252.7 7.2 fusion.130
  260.0 7.4 fusion.96
  267.5 6.8 psum.85
  274.3 11.7 %multiply_reduce_fusion.3 = (f32[512]{0:T(512)}, f32[2048,512]{1,0:T(8,128)}, bf16[2048,1,512]{2,0,1:T(8,128)(2,1)}) fusion(f32[2048,512]{1,0:T(8,128)} %get-tuple-element.766, f32[2048,2,512]{2,0,1:T(8,128)} %copy-done.1, f32[2048]{0:T(1024)S(1)} %broadcast_multiply_fusion.8, f32[2048,512]{1,0:T(8,128)} %get-tuple-element.762, ...), kind=kLoop, calls=%fused_computation.161 | loop fusion | flops 30408192 | bytes 25196544 | tf_op jit(solution)/shard_map/transpose(jvp())/reduce_sum | solution.py:83
  286.0 7.1 reshape.370
  293.1 6.8 copy.94
  305.2 198.0 %while.42 = (s32[]{:T(128)}, f32[8]{0:T(128)}, f32[8,64,128]{2,1,0:T(8,128)S(1)}, f32[8,256,8,64]{1,3,2,0:T(8,128)}, f32[8,256,8]{1,2,0:T(8,128)}, /*index=5*/f3...) while((s32[]{:T(128)}, f32[8]{0:T(128)}, ...), condition=%wide.region_24.25_spmd.clone, body=%wide.region_10.0_spmd.clone.sunk | while | flops 2126610432 | bytes 15952340 | solution.py:56
  337.4 3.4 fusion.252
  411.8 3.4 fusion.252
  503.2 6.9 copy.104
  510.1 7.5 reshape.371
  517.7 11.5 %multiply_reduce_fusion.6 = (f32[512]{0:T(512)S(1)}, f32[512]{0:T(512)S(1)}, f32[512]{0:T(512)S(1)}, f32[512]{0:T(512)S(1)}, f32[512]{0:T(512)S(1)}, /*index=5*/f32[2048,512]{1,0:T(8,128)S(1)}) fusion(f32[2048,512]{1,0:T(8,128)} %copy-done, f32[2048,2,512]{2,0,1:T(8,128)} %copy-done.1, f32[2048,512]{1,0:T(8,128)} %get-tuple-element.766, ...), kind=kLoop, calls=%fused_computation.164 | loop fusion | flops 20968960 | bytes 25178112 | tf_op jit(solution)/shard_map/transpose(jvp())/reduce_sum | solution.py:19
  529.2 5.8 broadcast_multiply_fusion
  535.0 7.1 fusion.127
  542.2 8.2 fusion.107
  554.3 6.8 bitcast_add_fusion
  562.4 7.8 fusion.148
  579.6 40.8 %all-reduce.21 = bf16[2048,256]{1,0:T(8,128)(2,1)S(1)} all-reduce(f32[2048,256]{1,0:T(8,128)S(1)} %pad_add_fusion.3), channel_id=1, replica_groups=mesh['dp'=8,'tensor'=4] {'tensor'}, use_global_device_ids=true, to_apply=%region_26.27 | all-reduce | flops 524288 | bytes 3145728 | tf_op jit(solution)/shard_map/psum | solution.py:195
  620.5 4.9 fusion.162
  628.7 8.8 reduce-scatter.11.cloned.1.call-done
  639.7 71.4 %reduce-scatter.9.cloned.1.call-done = f32[512,1024]{1,0:T(8,128)} async-done(((f32[2048,1024]{1,0:T(8,128)}), f32[512,1024]{1,0:T(8,128)}) %reduce-scatter.9.cloned.1.call-update) | async-done | bytes 2097168 | tf_op jit(solution)/shard_map/reduce_scatter | solution.py:206
  713.8 41.1 %all-reduce.19 = (f32[1024]{0:T(1024)}, f32[4,2048]{1,0:T(4,128)}, f32[2048]{0:T(1024)}, f32[4,256]{1,0:T(4,128)}, f32[256]{0:T(256)}, /*index=5*/f32[32]{0:T(128)}, f32[32]{0:T(128)}, f32[32]{0:T(128)}, f32[2048]{0:T(1024)}) all-reduce(f32[1024]{0:T(1024)S(1)} %get-tuple-element.689, ...), channel_id=1, replica_groups=mesh['dp'=8,'tensor'=4] {'dp','tensor'}, use_global_device_ids=true, to_apply=%region_29.30 | all-reduce | flops 14688 | bytes 117504 | tf_op jit(solution)/shard_map/psum | solution.py:225
  754.9 30.9 %reduce-scatter.7.cloned.1.call-done = f32[512,1024]{1,0:T(8,128)} async-done(((f32[2048,1024]{1,0:T(8,128)}), f32[512,1024]{1,0:T(8,128)}) %reduce-scatter.7.cloned.1.call-update) | async-done | bytes 2097168 | tf_op jit(solution)/shard_map/reduce_scatter | solution.py:159
  785.8 4.3 fusion.122
  790.0 54.2 %reduce-scatter.15.cloned.1.call-done = f32[128,8]{0,1:T(8,128)} async-done(((f32[1024,8]{0,1:T(8,128)}), f32[128,8]{0,1:T(8,128)}) %reduce-scatter.15.cloned.1.call-update) | async-done | bytes 4112 | tf_op jit(solution)/shard_map/reduce_scatter | solution.py:222
  844.3 67.1 %reduce-scatter.13.cloned.1.call-done = f32[128,256]{1,0:T(8,128)} async-done(((f32[1024,256]{1,0:T(8,128)}), f32[128,256]{1,0:T(8,128)}) %reduce-scatter.13.cloned.1.call-update) | async-done | bytes 131088 | tf_op jit(solution)/shard_map/reduce_scatter | solution.py:221
  (599 shorter events, 297.5 us)
Async XLA Ops:
  7.2 6.4 copy-start.52
  7.2 7.1 copy-start.55
  7.2 7.2 copy-start.56
  7.2 8.9 copy-start.48
  7.2 8.9 copy-start.49
  7.2 36.9 %copy-start.20 = (bf16[128,256]{1,0:T(8,128)(2,1)S(1)}, bf16[128,256]{1,0:T(8,128)(2,1)}, u32[]{:S(2)}) copy-start(bf16[128,256]{1,0:T(8,128)(2,1)} %param.23) | copy-start | bytes 196612
  7.3 70.3 %all-gather.6.cloned.1.call-start = ((), (), s32[]{:S(2)}) async-start(), calls=%async_computation.6 | async-start | bytes 5242880 | tf_op jit(solution)/shard_map/all_gather | solution.py:128
  8.9 7.3 copy-start.36
  8.9 7.3 copy-start.24
  11.4 90.1 %all-gather.8.cloned.1.call-start = ((), (), s32[]{:S(2)}) async-start(), calls=%async_computation.7 | async-start | bytes 2359296 | tf_op jit(solution)/shard_map/all_gather | solution.py:121
  12.2 240.5 %all-gather.12.cloned.1.call-start = ((), (), s32[]{:S(2)}) async-start(), calls=%async_computation.15 | async-start | bytes 5242880 | tf_op jit(solution)/shard_map/all_gather | solution.py:167
  13.0 247.0 %all-gather.10.cloned.1.call-start = ((), (), s32[]{:S(2)}) async-start(), calls=%async_computation.8 | async-start | bytes 1179648 | tf_op jit(solution)/shard_map/all_gather | solution.py:124
  13.6 613.3 %reduce-scatter.17.cloned.1.call-start = ((), (), s32[]{:S(2)}) async-start(), calls=%async_computation.14 | async-start | bytes 2359296 | tf_op jit(solution)/shard_map/reduce_scatter | solution.py:223
  15.2 259.0 %copy-start.26 = (f32[512]{0:T(512)}, f32[512]{0:T(512)S(1)}, u32[]{:S(2)}) copy-start(f32[512]{0:T(512)S(1)} %dynamic_slice.100) | copy-start | bytes 6148
  16.1 258.1 %copy-start.22 = (f32[512]{0:T(512)}, f32[512]{0:T(512)S(1)}, u32[]{:S(2)}) copy-start(f32[512]{0:T(512)S(1)} %mul.863) | copy-start | bytes 6148
  16.2 65.2 %copy-start.39 = (f32[1,256]{1,0:T(1,128)}, f32[1,256]{1,0:T(1,128)S(1)}, u32[]{:S(2)}) copy-start(f32[1,256]{1,0:T(1,128)S(1)} %get-tuple-element.793) | copy-start | bytes 3076
  16.2 65.2 %copy-start.41 = (f32[1,256]{1,0:T(1,128)}, f32[1,256]{1,0:T(1,128)S(1)}, u32[]{:S(2)}) copy-start(f32[1,256]{1,0:T(1,128)S(1)} %get-tuple-element.794) | copy-start | bytes 3076
  16.2 65.2 %copy-start.43 = (f32[1,256]{1,0:T(1,128)}, f32[1,256]{1,0:T(1,128)S(1)}, u32[]{:S(2)}) copy-start(f32[1,256]{1,0:T(1,128)S(1)} %get-tuple-element.795) | copy-start | bytes 3076
  16.2 65.2 %copy-start.45 = (f32[1,256]{1,0:T(1,128)}, f32[1,256]{1,0:T(1,128)S(1)}, u32[]{:S(2)}) copy-start(f32[1,256]{1,0:T(1,128)S(1)} %get-tuple-element.796) | copy-start | bytes 3076
  44.1 86.8 %copy-start.18 = (bf16[1024,8]{0,1:T(8,128)(2,1)}, bf16[1024,8]{0,1:T(8,128)(2,1)S(1)}, u32[]{:S(2)}) copy-start(bf16[1024,8]{0,1:T(8,128)(2,1)S(1)} %all_gather.19) | copy-start | bytes 49156
  44.2 37.3 %copy-start.51 = (f32[256]{0:T(256)S(1)}, f32[256]{0:T(256)}, u32[]{:S(2)}) copy-start(f32[256]{0:T(256)} %param.29) | copy-start | bytes 3076
  76.6 4.8 copy-start.10
  77.5 34.7 %copy-start.28 = (f32[1,512]{1,0:T(1,128)}, f32[1,512]{1,0:T(1,128)S(1)}, u32[]{:S(2)}) copy-start(f32[1,512]{1,0:T(1,128)S(1)} %get-tuple-element.787) | copy-start | bytes 6148
  77.5 34.7 %copy-start.30 = (f32[1,512]{1,0:T(1,128)}, f32[1,512]{1,0:T(1,128)S(1)}, u32[]{:S(2)}) copy-start(f32[1,512]{1,0:T(1,128)S(1)} %get-tuple-element.788) | copy-start | bytes 6148
  77.6 34.7 %copy-start.32 = (f32[1,512]{1,0:T(1,128)}, f32[1,512]{1,0:T(1,128)S(1)}, u32[]{:S(2)}) copy-start(f32[1,512]{1,0:T(1,128)S(1)} %get-tuple-element.789) | copy-start | bytes 6148
  77.6 34.7 %copy-start.34 = (f32[1,512]{1,0:T(1,128)}, f32[1,512]{1,0:T(1,128)S(1)}, u32[]{:S(2)}) copy-start(f32[1,512]{1,0:T(1,128)S(1)} %get-tuple-element.790) | copy-start | bytes 6148
  112.3 4.7 copy-start
  252.7 21.6 %copy-start.16 = (f32[2048]{0:T(1024)}, f32[2048]{0:T(1024)S(1)}, u32[]{:S(2)}) copy-start(f32[2048]{0:T(1024)S(1)} %get-tuple-element.792) | copy-start | bytes 24580
  260.0 377.4 %reduce-scatter.11.cloned.1.call-start = ((), (), s32[]{:S(2)}) async-start(), calls=%async_computation.11 | async-start | bytes 4718592 | tf_op jit(solution)/shard_map/reduce_scatter | solution.py:220
  510.1 7.5 copy-start.23
  517.6 11.6 %copy-start.29 = (f32[1,512]{1,0:T(1,128)S(1)}, f32[1,512]{1,0:T(1,128)}, u32[]{:S(2)}) copy-start(f32[1,512]{1,0:T(1,128)} %copy-done.28) | copy-start | bytes 6148
  517.6 11.6 %copy-start.31 = (f32[1,512]{1,0:T(1,128)S(1)}, f32[1,512]{1,0:T(1,128)}, u32[]{:S(2)}) copy-start(f32[1,512]{1,0:T(1,128)} %copy-done.30) | copy-start | bytes 6148
  517.6 11.6 %copy-start.33 = (f32[1,512]{1,0:T(1,128)S(1)}, f32[1,512]{1,0:T(1,128)}, u32[]{:S(2)}) copy-start(f32[1,512]{1,0:T(1,128)} %copy-done.32) | copy-start | bytes 6148
  517.6 11.6 %copy-start.35 = (f32[1,512]{1,0:T(1,128)S(1)}, f32[1,512]{1,0:T(1,128)}, u32[]{:S(2)}) copy-start(f32[1,512]{1,0:T(1,128)} %copy-done.34) | copy-start | bytes 6148
  535.0 7.2 copy-start.2
  550.4 160.6 %reduce-scatter.9.cloned.1.call-start = ((), (), s32[]{:S(2)}) async-start(), calls=%async_computation.10 | async-start | bytes 10485760 | tf_op jit(solution)/shard_map/reduce_scatter | solution.py:206
  561.2 224.6 %reduce-scatter.7.cloned.1.call-start = ((), (), s32[]{:S(2)}) async-start(), calls=%async_computation.9 | async-start | bytes 10485760 | tf_op jit(solution)/shard_map/reduce_scatter | solution.py:159
  570.2 274.0 %reduce-scatter.15.cloned.1.call-start = ((), (), s32[]{:S(2)}) async-start(), calls=%async_computation.13 | async-start | bytes 36864 | tf_op jit(solution)/shard_map/reduce_scatter | solution.py:222
  620.4 5.1 copy-start.11
  620.4 5.1 copy-start.47
  620.4 5.1 copy-start.50
  620.4 6.2 copy-start.38
  620.4 6.2 copy-start.53
  620.4 90.6 %copy-start.4 = (bf16[1,512,1024]{2,1,0:T(8,128)(2,1)S(1)}, bf16[1,512,1024]{2,1,0:T(8,128)(2,1)}, u32[]{:S(2)}) copy-start(bf16[1,512,1024]{2,1,0:T(8,128)(2,1)} %param.19) | copy-start | bytes 3145732
  620.5 90.6 %copy-start.21 = (f32[1024]{0:T(1024)S(1)}, f32[1024]{0:T(1024)}, u32[]{:S(2)}) copy-start(f32[1024]{0:T(1024)} %param.21) | copy-start | bytes 12292
  620.5 90.6 %copy-start.25 = (f32[512]{0:T(512)S(1)}, f32[512]{0:T(512)}, u32[]{:S(2)}) copy-start(f32[512]{0:T(512)} %copy-done.24) | copy-start | bytes 6148
  620.5 290.9 %reduce-scatter.13.cloned.1.call-start = ((), (), s32[]{:S(2)}) async-start(), calls=%async_computation.12 | async-start | bytes 1179648 | tf_op jit(solution)/shard_map/reduce_scatter | solution.py:221
  625.4 129.5 %copy-start.37 = (f32[512]{0:T(512)S(1)}, f32[512]{0:T(512)}, u32[]{:S(2)}) copy-start(f32[512]{0:T(512)} %copy-done.36) | copy-start | bytes 6148
  (19 other events, 43.6 us)
Sparse Core Ops, SparseCore 0:
  11.6 37.1 all-gather.5
  51.5 49.9 all-gather.7
  103.1 32.9 all-gather.11
  138.1 40.3 all-gather.9
  260.1 68.2 reduce-scatter.16
  550.6 86.8 reduce-scatter.10
  640.0 71.0 reduce-scatter.8
  713.6 72.0 reduce-scatter.6
  789.5 54.7 reduce-scatter.14
  848.1 63.1 reduce-scatter.12
where the time goes:
time: 926 us; the launch traced here: 919 us
  waiting for transfers between devices  249 us (27%)
  matrix products  235 us (25%)
  blocking collectives  155 us (17%)
  other arithmetic  140 us (15%)
  local copies, waits for them, and re-layouts  123 us (13%)
  between operations  15.3 us (2%)
    dot_general x24, matrix products, step_block(): jnp.einsum('ijh,jhp->ihp', weights, x_block, precision=FULL_PRECISION)  78.3 us
    reduce_scatter x1, waiting for transfers between devices, body(): lax.psum_scatter(from_zx + lax.dot_general(grad_dt_low, dt_full, CONTRACT...  71.4 us
    reduce_scatter x1, waiting for transfers between devices, body(): lax.psum_scatter(grad_bc_w, 'dp', scatter_dimension=0, tiled=True)  67.1 us
    reduce_scatter x1, waiting for transfers between devices, body(): lax.psum_scatter(grad_dt_w, 'dp', scatter_dimension=0, tiled=True)  54.2 us
    psum x1, blocking collectives, body(): lax.psum((grad_norm_gain, widen(grad_x_taps, chan_start, total_channels),...  41.1 us
    psum x1, blocking collectives, body(): grad_bc_in = lax.psum(grad_bc_part, 'tensor').astype(jnp.bfloat16)  40.8 us
    another operation x73, other arithmetic  39.1 us
    dot_general x32, matrix products, step_block(): jnp.einsum('in,hpn->ihp', c_block, state, precision=FULL_PRECISION)  35.8 us
  transfers between devices with their start and end apart: 10, of which 6 were waited for; matrix products, arithmetic and copies ran while one was open for 53% of the time, Pallas kernels for 0%

commit v1 on v0

--- a/solution.py
+++ b/solution.py
@@ -8,6 +8,22 @@
 FULL_PRECISION = lax.Precision.HIGHEST
 CONTRACT_LAST = (((1,), (1,)), ((), ()))
 CONTRACT_FIRST = (((0,), (0,)), ((), ()))
+
+
+def collect(x, axis, dim):
+    ways, here, step = (lax.axis_size(axis), lax.axis_index(axis), x.shape[dim])
+    shape = [n * ways if d == dim else n for d, n in enumerate(x.shape)]
+    full = lax.dynamic_update_slice_in_dim(jnp.zeros(shape, x.dtype), x, here * step, axis=dim)
+    going_up = going_down = x
+    for far in range(1, ways // 2 + 1):
+        going_up = lax.ppermute(going_up, axis, [(d, (d + 1) % ways) for d in range(ways)])
+        full = lax.dynamic_update_slice_in_dim(full, going_up, (here - far) % ways * step, axis=dim)
+        if 2 * far < ways:
+            going_down = lax.ppermute(going_down, axis, [(d, (d - 1) % ways) for d in range(ways)])
+            full = lax.dynamic_update_slice_in_dim(
+                full, going_down, (here + far) % ways * step, axis=dim
+            )
+    return full
 
 
 def causal_conv(values, conv_taps):
@@ -120,7 +136,7 @@
     zx_full, bc_full, dt_full, out_full = (
         lax.all_gather(w_zx, "dp", axis=0, tiled=True),
         lax.all_gather(w_bc, "dp", axis=0, tiled=True),
-        lax.all_gather(w_dt, "dp", axis=0, tiled=True),
+        collect(w_dt, "dp", 0),
         lax.all_gather(w_out, "dp", axis=0, tiled=True),
     )
     acts_row = acts[0].astype(jnp.float32)

time: 926 us -> 925 us (level)
  blocking collectives: 155 us -> 126 us
  starting transfers between devices: 0.66 us -> 16.4 us
    all_gather x1 -> x0, blocking collectives: 27.9 us -> none  [body(): lax.all_gather(w_dt, 'dp', axis=0, tiled=True)]
    ppermute x0 -> x7, starting transfers between devices: none -> 15.4 us  [the longest x3 15.4 us: collect(): lax.ppermute(going_down, axis, [(d, (d - 1) % ways) for d in range(ways)])]
    ppermute x0 -> x7, waiting for transfers between devices: none -> 13.9 us  [the longest x4 12.6 us: collect(): lax.ppermute(going_up, axis, [(d, (d + 1) % ways) for d in range(ways)])]
    unnamed x119 -> x117, local copies, waits for them, and re-layouts: 28.6 us -> 27.7 us
  transfers between devices with their start and end apart: 10 -> 17, of which waited for: 6 -> 10; matrix products, arithmetic and copies ran while one was open for 53% -> 53% of each run, Pallas kernels for 0% -> 0%
where the time goes in v1:
time: 925 us; the launch traced here: 918 us
  waiting for transfers between devices  257 us (28%)
  matrix products  240 us (26%)
  other arithmetic  140 us (15%)
  blocking collectives  126 us (14%)
  local copies, waits for them, and re-layouts  122 us (13%)
  starting transfers between devices  16.4 us (2%)
  between operations  15.6 us (2%)
    dot_general x24, matrix products, step_block(): jnp.einsum('ijh,jhp->ihp', weights, x_block, precision=FULL_PRECISION)  78.3 us
    reduce_scatter x1, waiting for transfers between devices, body(): lax.psum_scatter(from_zx + lax.dot_general(grad_dt_low, dt_full, CONTRACT...  71.4 us
    reduce_scatter x1, waiting for transfers between devices, body(): lax.psum_scatter(grad_bc_w, 'dp', scatter_dimension=0, tiled=True)  67.1 us
    reduce_scatter x1, waiting for transfers between devices, body(): lax.psum_scatter(grad_dt_w, 'dp', scatter_dimension=0, tiled=True)  53.5 us
    psum x1, blocking collectives, body(): lax.psum((grad_norm_gain, widen(grad_x_taps, chan_start, total_channels),...  41.1 us
    psum x1, blocking collectives, body(): grad_bc_in = lax.psum(grad_bc_part, 'tensor').astype(jnp.bfloat16)  40.6 us
    another operation x73, other arithmetic  39.1 us
    dot_general x32, matrix products, step_block(): jnp.einsum('in,hpn->ihp', c_block, state, precision=FULL_PRECISION)  35.8 us
  transfers between devices with their start and end apart: 17, of which 10 were waited for; matrix products, arithmetic and copies ran while one was open for 53% of the time, Pallas kernels for 0%

profile of v1, /device:TPU:0, one launch (start us, length us, event | category | flops | bytes accessed | tf_op | source)
XLA Modules:
  0.0 917.9 jit_solution(10180058066860977953)
XLA Ops:
  13.0 6.1 collective-permute-start.1
  20.1 31.6 %all_gather.17 = bf16[1024,256]{1,0:T(8,128)(2,1)S(1)} all-gather(bf16[128,256]{1,0:T(8,128)(2,1)S(1)} %copy-done.20), channel_id=1, replica_groups=mesh['dp'=8,'tensor'=4] {'dp'}, dimensions={0}, use_global_device_ids=true | all-gather | bytes 589824 | tf_op jit(solution)/shard_map/all_gather | solution.py:138
  54.7 4.4 collective-permute-start.3
  60.4 5.0 collective-permute-start.5
  65.4 6.3 collective-permute-done.4
  71.7 6.3 collective-permute-done.6
  86.5 14.2 %all-gather.8.cloned.1.call-done = bf16[1024,2,512]{2,0,1:T(8,128)(2,1)} async-done(((bf16[128,2,512]{2,0,1:T(8,128)(2,1)}), bf16[1024,2,512]{2,0,1:T(8,128)(2,1)}) %all-gather.8.cloned.1.call-update) | async-done | bytes 2097168 | tf_op jit(solution)/shard_map/all_gather | solution.py:137
  100.7 7.1 fusion.109
  111.4 4.6 fusion.124
  116.1 7.1 reshape.372
  123.2 6.9 copy.89
  130.1 4.0 compare_select_fusion.2
  136.6 87.6 %while.43 = (s32[]{:T(128)}, f32[8,64,128]{2,1,0:T(8,128)S(1)}, f32[8,256,8,64]{1,3,2,0:T(8,128)}, f32[8,8,64,128]{3,2,1,0:T(8,128)}, f32[8,256,8]{1,2,0:T(8,128...) while((s32[]{:T(128)}, f32[8,64,128]{2,1,0:T(8,128)S(1)}, ...), condition=%wide.region_4.5_spmd.clone.clone, body=%wide.region_1.4_spmd.clone.clone.sunk | while | flops 909711360 | bytes 5641051 | solution.py:72
  139.1 3.6 fusion.271
  150.1 3.6 fusion.271
  161.1 3.6 fusion.271
  204.9 3.6 fusion.271
  215.8 3.6 fusion.271
  224.2 6.9 copy.101
  231.1 7.5 reshape.369
  238.6 7.5 multiply_reduce_fusion.8
  246.1 5.7 psum.84
  251.9 7.2 fusion.131
  259.2 7.4 fusion.96
  266.6 6.7 psum.85
  273.4 11.7 %multiply_reduce_fusion.3 = (f32[512]{0:T(512)}, f32[2048,512]{1,0:T(8,128)}, bf16[2048,1,512]{2,0,1:T(8,128)(2,1)}) fusion(f32[2048,512]{1,0:T(8,128)} %get-tuple-element.766, f32[2048,2,512]{2,0,1:T(8,128)} %copy-done.1, f32[2048]{0:T(1024)S(1)} %broadcast_multiply_fusion.8, f32[2048,512]{1,0:T(8,128)} %get-tuple-element.762, ...), kind=kLoop, calls=%fused_computation.161 | loop fusion | flops 30408192 | bytes 25196544 | tf_op jit(solution)/shard_map/transpose(jvp())/reduce_sum | solution.py:99
  285.1 7.1 reshape.370
  292.2 6.8 copy.94
  304.3 198.0 %while.42 = (s32[]{:T(128)}, f32[8]{0:T(128)}, f32[8,64,128]{2,1,0:T(8,128)S(1)}, f32[8,256,8,64]{1,3,2,0:T(8,128)}, f32[8,256,8]{1,2,0:T(8,128)}, /*index=5*/f3...) while((s32[]{:T(128)}, f32[8]{0:T(128)}, ...), condition=%wide.region_24.25_spmd.clone, body=%wide.region_10.24_spmd.clone.sunk | while | flops 2126610432 | bytes 15952340 | solution.py:72
  502.3 6.9 copy.104
  509.2 7.5 reshape.371
  516.8 11.6 %multiply_reduce_fusion.6 = (f32[512]{0:T(512)S(1)}, f32[512]{0:T(512)S(1)}, f32[512]{0:T(512)S(1)}, f32[512]{0:T(512)S(1)}, f32[512]{0:T(512)S(1)}, /*index=5*/f32[2048,512]{1,0:T(8,128)S(1)}) fusion(f32[2048,512]{1,0:T(8,128)} %copy-done, f32[2048,2,512]{2,0,1:T(8,128)} %copy-done.1, f32[2048,512]{1,0:T(8,128)} %get-tuple-element.766, ...), kind=kLoop, calls=%fused_computation.164 | loop fusion | flops 20968960 | bytes 25178112 | tf_op jit(solution)/shard_map/transpose(jvp())/reduce_sum | solution.py:35
  528.4 5.7 broadcast_multiply_fusion
  534.1 7.1 fusion.128
  541.3 8.3 fusion.107
  551.2 6.9 fusion.115
  558.1 4.5 bitcast_add_fusion
  563.9 7.8 fusion.149
  581.0 40.6 %all-reduce.21 = bf16[2048,256]{1,0:T(8,128)(2,1)S(1)} all-reduce(f32[2048,256]{1,0:T(8,128)S(1)} %pad_add_fusion.3), channel_id=1, replica_groups=mesh['dp'=8,'tensor'=4] {'tensor'}, use_global_device_ids=true, to_apply=%region_26.27 | all-reduce | flops 524288 | bytes 3145728 | tf_op jit(solution)/shard_map/psum | solution.py:211
  622.1 4.8 fusion.163
  630.1 6.5 reduce-scatter.11.cloned.1.call-done
  638.8 71.4 %reduce-scatter.9.cloned.1.call-done = f32[512,1024]{1,0:T(8,128)} async-done(((f32[2048,1024]{1,0:T(8,128)}), f32[512,1024]{1,0:T(8,128)}) %reduce-scatter.9.cloned.1.call-update) | async-done | bytes 2097168 | tf_op jit(solution)/shard_map/reduce_scatter | solution.py:222
  710.3 4.0 fusion.119
  714.3 41.1 %all-reduce.19 = (f32[1024]{0:T(1024)}, f32[4,2048]{1,0:T(4,128)}, f32[2048]{0:T(1024)}, f32[4,256]{1,0:T(4,128)}, f32[256]{0:T(256)}, /*index=5*/f32[32]{0:T(128)}, f32[32]{0:T(128)}, f32[32]{0:T(128)}, f32[2048]{0:T(1024)}) all-reduce(f32[1024]{0:T(1024)S(1)} %get-tuple-element.683, ...), channel_id=1, replica_groups=mesh['dp'=8,'tensor'=4] {'dp','tensor'}, use_global_device_ids=true, to_apply=%region_29.30 | all-reduce | flops 14688 | bytes 117504 | tf_op jit(solution)/shard_map/psum | solution.py:241
  755.4 29.5 %reduce-scatter.7.cloned.1.call-done = f32[512,1024]{1,0:T(8,128)} async-done(((f32[2048,1024]{1,0:T(8,128)}), f32[512,1024]{1,0:T(8,128)}) %reduce-scatter.7.cloned.1.call-update) | async-done | bytes 2097168 | tf_op jit(solution)/shard_map/reduce_scatter | solution.py:175
  785.0 5.0 fusion.123
  790.0 53.5 %reduce-scatter.15.cloned.1.call-done = f32[128,8]{0,1:T(8,128)} async-done(((f32[1024,8]{0,1:T(8,128)}), f32[128,8]{0,1:T(8,128)}) %reduce-scatter.15.cloned.1.call-update) | async-done | bytes 4112 | tf_op jit(solution)/shard_map/reduce_scatter | solution.py:238
  843.5 67.1 %reduce-scatter.13.cloned.1.call-done = f32[128,256]{1,0:T(8,128)} async-done(((f32[1024,256]{1,0:T(8,128)}), f32[128,256]{1,0:T(8,128)}) %reduce-scatter.13.cloned.1.call-update) | async-done | bytes 131088 | tf_op jit(solution)/shard_map/reduce_scatter | solution.py:237
  (619 shorter events, 315.1 us)
Async XLA Ops:
  7.2 12.1 %copy-start.52 = (f32[32]{0:T(128)S(1)}, f32[32]{0:T(128)}, u32[]{:S(2)}) copy-start(f32[32]{0:T(128)} %param.31) | copy-start | bytes 388
  7.2 12.8 %copy-start.48 = (f32[4,256]{1,0:T(4,128)S(1)}, f32[4,256]{1,0:T(4,128)}, u32[]{:S(2)}) copy-start(f32[4,256]{1,0:T(4,128)} %param.28) | copy-start | bytes 12292
  7.2 12.8 %copy-start.20 = (bf16[128,256]{1,0:T(8,128)(2,1)S(1)}, bf16[128,256]{1,0:T(8,128)(2,1)}, u32[]{:S(2)}) copy-start(bf16[128,256]{1,0:T(8,128)(2,1)} %param.23) | copy-start | bytes 196612
  7.2 45.6 %copy-start.54 = (f32[32]{0:T(128)S(1)}, f32[32]{0:T(128)}, u32[]{:S(2)}) copy-start(f32[32]{0:T(128)} %param.30) | copy-start | bytes 388
  7.2 45.7 %copy-start.55 = (f32[32]{0:T(128)S(1)}, f32[32]{0:T(128)}, u32[]{:S(2)}) copy-start(f32[32]{0:T(128)} %param.32) | copy-start | bytes 388
  7.3 70.7 %all-gather.6.cloned.1.call-start = ((), (), s32[]{:S(2)}) async-start(), calls=%async_computation.6 | async-start | bytes 5242880 | tf_op jit(solution)/shard_map/all_gather | solution.py:144
  8.9 11.1 %copy-start.36 = (f32[512]{0:T(512)}, f32[512]{0:T(512)S(1)}, u32[]{:S(2)}) copy-start(f32[512]{0:T(512)S(1)} %fusion.125) | copy-start | bytes 6148
  8.9 11.1 %copy-start.24 = (f32[512]{0:T(512)}, f32[512]{0:T(512)S(1)}, u32[]{:S(2)}) copy-start(f32[512]{0:T(512)S(1)} %fusion.145) | copy-start | bytes 6148
  11.4 89.2 %all-gather.8.cloned.1.call-start = ((), (), s32[]{:S(2)}) async-start(), calls=%async_computation.7 | async-start | bytes 2359296 | tf_op jit(solution)/shard_map/all_gather | solution.py:137
  12.2 239.6 %all-gather.12.cloned.1.call-start = ((), (), s32[]{:S(2)}) async-start(), calls=%async_computation.15 | async-start | bytes 5242880 | tf_op jit(solution)/shard_map/all_gather | solution.py:183
  13.0 246.2 %all-gather.10.cloned.1.call-start = ((), (), s32[]{:S(2)}) async-start(), calls=%async_computation.8 | async-start | bytes 1179648 | tf_op jit(solution)/shard_map/all_gather | solution.py:140
  13.0 41.6 %collective-permute-start.1 = (bf16[128,8]{0,1:T(8,128)(2,1)S(1)}, bf16[128,8]{0,1:T(8,128)(2,1)S(1)}, u32[]{:S(2)}, u32[]{:S(2)}) collective-permute-start(bf16[128,8]{0,1:T(8,128)(2,1)S(1)} %copy-done.49), channel_id=1, source_target_pairs={{0,28},{4,0},{8,4},{12,8},{16,12},{20,16},{24,20},{28,24},{1,29},{... | collective-permute-start | bytes 6152 | tf_op jit(solution)/shard_map/ppermute | solution.py:22
  19.1 39.9 %collective-permute-start = (bf16[128,8]{0,1:T(8,128)(2,1)S(1)}, bf16[128,8]{0,1:T(8,128)(2,1)S(1)}, u32[]{:S(2)}, u32[]{:S(2)}) collective-permute-start(bf16[128,8]{0,1:T(8,128)(2,1)S(1)} %copy-done.49), channel_id=1, source_target_pairs={{0,4},{4,8},{8,12},{12,16},{16,20},{20,24},{24,28},{28,0},{1,5},{5... | collective-permute-start | bytes 6152 | tf_op jit(solution)/shard_map/ppermute | solution.py:19
  19.2 609.2 %reduce-scatter.17.cloned.1.call-start = ((), (), s32[]{:S(2)}) async-start(), calls=%async_computation.14 | async-start | bytes 2359296 | tf_op jit(solution)/shard_map/reduce_scatter | solution.py:239
  20.0 61.6 %copy-start.39 = (f32[1,256]{1,0:T(1,128)}, f32[1,256]{1,0:T(1,128)S(1)}, u32[]{:S(2)}) copy-start(f32[1,256]{1,0:T(1,128)S(1)} %get-tuple-element.793) | copy-start | bytes 3076
  20.0 61.6 %copy-start.41 = (f32[1,256]{1,0:T(1,128)}, f32[1,256]{1,0:T(1,128)S(1)}, u32[]{:S(2)}) copy-start(f32[1,256]{1,0:T(1,128)S(1)} %get-tuple-element.794) | copy-start | bytes 3076
  20.0 61.6 %copy-start.43 = (f32[1,256]{1,0:T(1,128)}, f32[1,256]{1,0:T(1,128)S(1)}, u32[]{:S(2)}) copy-start(f32[1,256]{1,0:T(1,128)S(1)} %get-tuple-element.795) | copy-start | bytes 3076
  20.1 61.6 %copy-start.45 = (f32[1,256]{1,0:T(1,128)}, f32[1,256]{1,0:T(1,128)S(1)}, u32[]{:S(2)}) copy-start(f32[1,256]{1,0:T(1,128)S(1)} %get-tuple-element.796) | copy-start | bytes 3076
  20.1 61.6 %copy-start.51 = (f32[256]{0:T(256)S(1)}, f32[256]{0:T(256)}, u32[]{:S(2)}) copy-start(f32[256]{0:T(256)} %param.29) | copy-start | bytes 3076
  51.7 29.9 %copy-start.10 = (bf16[1024,256]{1,0:T(8,128)(2,1)}, bf16[1024,256]{1,0:T(8,128)(2,1)S(1)}, u32[]{:S(2)}) copy-start(bf16[1024,256]{1,0:T(8,128)(2,1)S(1)} %all_gather.17) | copy-start | bytes 1572868
  52.7 58.7 %copy-start.28 = (f32[1,512]{1,0:T(1,128)}, f32[1,512]{1,0:T(1,128)S(1)}, u32[]{:S(2)}) copy-start(f32[1,512]{1,0:T(1,128)S(1)} %get-tuple-element.787) | copy-start | bytes 6148
  52.7 58.7 %copy-start.30 = (f32[1,512]{1,0:T(1,128)}, f32[1,512]{1,0:T(1,128)S(1)}, u32[]{:S(2)}) copy-start(f32[1,512]{1,0:T(1,128)S(1)} %get-tuple-element.788) | copy-start | bytes 6148
  52.7 58.7 %copy-start.32 = (f32[1,512]{1,0:T(1,128)}, f32[1,512]{1,0:T(1,128)S(1)}, u32[]{:S(2)}) copy-start(f32[1,512]{1,0:T(1,128)S(1)} %get-tuple-element.789) | copy-start | bytes 6148
  52.8 58.7 %copy-start.34 = (f32[1,512]{1,0:T(1,128)}, f32[1,512]{1,0:T(1,128)S(1)}, u32[]{:S(2)}) copy-start(f32[1,512]{1,0:T(1,128)S(1)} %get-tuple-element.790) | copy-start | bytes 6148
  53.8 219.6 %copy-start.26 = (f32[512]{0:T(512)}, f32[512]{0:T(512)S(1)}, u32[]{:S(2)}) copy-start(f32[512]{0:T(512)S(1)} %dynamic_slice.100) | copy-start | bytes 6148
  54.7 218.7 %copy-start.22 = (f32[512]{0:T(512)}, f32[512]{0:T(512)S(1)}, u32[]{:S(2)}) copy-start(f32[512]{0:T(512)S(1)} %mul.895) | copy-start | bytes 6148
  54.7 5.7 collective-permute-start.3
  59.1 6.3 collective-permute-start.2
  60.4 11.3 %collective-permute-start.5 = (bf16[128,8]{0,1:T(8,128)(2,1)S(1)}, bf16[128,8]{0,1:T(8,128)(2,1)S(1)}, u32[]{:S(2)}, u32[]{:S(2)}) collective-permute-start(bf16[128,8]{0,1:T(8,128)(2,1)S(1)} %collective-permute-done.3), channel_id=1, source_target_pairs={{0,28},{4,0},{8,4},{12,8},{16,12},{20,16},{24,20},{28,24},{1,29},{... | collective-permute-start | bytes 6152 | tf_op jit(solution)/shard_map/ppermute | solution.py:22
  65.4 6.3 collective-permute-start.4
  71.7 6.3 collective-permute-start.6
  78.0 52.1 %copy-start.18 = (bf16[1024,8]{0,1:T(8,128)(2,1)}, bf16[1024,8]{0,1:T(8,128)(2,1)S(1)}, u32[]{:S(2)}) copy-start(bf16[1024,8]{0,1:T(8,128)(2,1)S(1)} %constant_dynamic-update-slice_fusion) | copy-start | bytes 49156
  251.9 21.5 %copy-start.16 = (f32[2048]{0:T(1024)}, f32[2048]{0:T(1024)S(1)}, u32[]{:S(2)}) copy-start(f32[2048]{0:T(1024)S(1)} %get-tuple-element.792) | copy-start | bytes 24580
  259.1 377.4 %reduce-scatter.11.cloned.1.call-start = ((), (), s32[]{:S(2)}) async-start(), calls=%async_computation.11 | async-start | bytes 4718592 | tf_op jit(solution)/shard_map/reduce_scatter | solution.py:236
  509.2 7.5 copy-start.23
  516.8 11.6 %copy-start.29 = (f32[1,512]{1,0:T(1,128)S(1)}, f32[1,512]{1,0:T(1,128)}, u32[]{:S(2)}) copy-start(f32[1,512]{1,0:T(1,128)} %copy-done.28) | copy-start | bytes 6148
  516.8 11.6 %copy-start.31 = (f32[1,512]{1,0:T(1,128)S(1)}, f32[1,512]{1,0:T(1,128)}, u32[]{:S(2)}) copy-start(f32[1,512]{1,0:T(1,128)} %copy-done.30) | copy-start | bytes 6148
  516.8 11.6 %copy-start.33 = (f32[1,512]{1,0:T(1,128)S(1)}, f32[1,512]{1,0:T(1,128)}, u32[]{:S(2)}) copy-start(f32[1,512]{1,0:T(1,128)} %copy-done.32) | copy-start | bytes 6148
  516.8 11.6 %copy-start.35 = (f32[1,512]{1,0:T(1,128)S(1)}, f32[1,512]{1,0:T(1,128)}, u32[]{:S(2)}) copy-start(f32[1,512]{1,0:T(1,128)} %copy-done.34) | copy-start | bytes 6148
  549.6 160.7 %reduce-scatter.9.cloned.1.call-start = ((), (), s32[]{:S(2)}) async-start(), calls=%async_computation.10 | async-start | bytes 10485760 | tf_op jit(solution)/shard_map/reduce_scatter | solution.py:222
  562.7 222.3 %reduce-scatter.7.cloned.1.call-start = ((), (), s32[]{:S(2)}) async-start(), calls=%async_computation.9 | async-start | bytes 10485760 | tf_op jit(solution)/shard_map/reduce_scatter | solution.py:175
  571.7 271.8 %reduce-scatter.15.cloned.1.call-start = ((), (), s32[]{:S(2)}) async-start(), calls=%async_computation.13 | async-start | bytes 36864 | tf_op jit(solution)/shard_map/reduce_scatter | solution.py:238
  621.7 88.6 %copy-start.4 = (bf16[1,512,1024]{2,1,0:T(8,128)(2,1)S(1)}, bf16[1,512,1024]{2,1,0:T(8,128)(2,1)}, u32[]{:S(2)}) copy-start(bf16[1,512,1024]{2,1,0:T(8,128)(2,1)} %param.19) | copy-start | bytes 3145732
  621.7 88.5 %copy-start.21 = (f32[1024]{0:T(1024)S(1)}, f32[1024]{0:T(1024)}, u32[]{:S(2)}) copy-start(f32[1024]{0:T(1024)} %param.21) | copy-start | bytes 12292
  621.7 88.5 %copy-start.25 = (f32[512]{0:T(512)S(1)}, f32[512]{0:T(512)}, u32[]{:S(2)}) copy-start(f32[512]{0:T(512)} %copy-done.24) | copy-start | bytes 6148
  621.7 288.9 %reduce-scatter.13.cloned.1.call-start = ((), (), s32[]{:S(2)}) async-start(), calls=%async_computation.12 | async-start | bytes 1179648 | tf_op jit(solution)/shard_map/reduce_scatter | solution.py:237
  626.9 128.5 %copy-start.37 = (f32[512]{0:T(512)S(1)}, f32[512]{0:T(512)}, u32[]{:S(2)}) copy-start(f32[512]{0:T(512)} %copy-done.36) | copy-start | bytes 6148
  710.3 74.7 %copy-start.5 = (f32[512,1024]{1,0:T(8,128)S(1)}, f32[512,1024]{1,0:T(8,128)}, u32[]{:S(2)}) copy-start(f32[512,1024]{1,0:T(8,128)} %reduce-scatter.9.cloned.1.call-done) | copy-start | bytes 6291460
  (25 other events, 91.0 us)
Sparse Core Ops, SparseCore 0:
  11.6 37.1 all-gather.5
  51.5 49.0 all-gather.7
  102.2 32.9 all-gather.11
  137.2 40.3 all-gather.9
  259.3 68.0 reduce-scatter.16
  549.7 86.8 reduce-scatter.10
  639.2 71.0 reduce-scatter.8
  712.8 72.1 reduce-scatter.6
  788.7 54.7 reduce-scatter.14
  847.3 63.2 reduce-scatter.12
